TPU v7x, 256 devices: a whole 4x4x8 slice. The times are simulated.
256 devices in a mesh: dp: 64 (over x, z, core), tensor: 4 (over y).
Axes of the slice: x: 4, y: 4, z: 8, core: 2. Of those that a mesh axis runs over, the one named last changes fastest.
Arguments:
- activations: bfloat16 [768, 8192], P('dp', 'tensor'), may hold values from -400 to 400, as said below
- weight: bfloat16 [8192, 28672], P('dp', 'tensor'), may hold values from -0.0625 to 0.0625
Outputs:
- channel_mean: float32 [8192], P('dp')
- column_errors: float32 [4, 28672], P(None, ('tensor', 'dp'))
- errors: float32 [4], replicated
Inputs may be any that keep to these rules, and one draw needn't show every extreme that they name: activations and weight are finite real values within the ranges stated above.
All inputs are finite; a program needn't handle non-finite values.
Results may differ from a plain program's by a relative error of at most 0.0012.
The roundings to bfloat16 on the way count: a program that leaves them out, or rounds other values in their place, can miss the bound.
Values may be sent and summed in bfloat16 or wider, within the bound.
A program may use at most 128 MiB of HBM per device.

v0:
```python
import functools
import math
import jax
import jax.numpy as jnp
from jax import lax
from jax.sharding import Mesh
from jax.sharding import PartitionSpec as P

D = 8192
F = 28672
GROUP = 128
GRID = 4
DP = ("dp_0", "dp_1", "dp_2")
DP_TENSOR = ("dp_0", "dp_1", "dp_2", "tensor")
TENSOR_DP = ("tensor", "dp_0", "dp_1", "dp_2")


def laid_out(parts, dim):
    parts = jnp.moveaxis(parts, 0, dim)
    dims = parts.shape
    return parts.reshape(*dims[:dim], dims[dim] * dims[dim + 1], *dims[dim + 2 :])


def from_everyone(shard, axis):
    devices = lax.axis_size(axis)
    return lax.all_to_all(
        jnp.broadcast_to(shard[None], (devices, *shard.shape)), axis, 0, 0, tiled=True
    )


def gather_directly(shard, axis, dim):
    return laid_out(from_everyone(shard, axis), dim)


def by_axis(shard, axes):
    return functools.reduce(lax.psum, axes, shard)


def soft_round(values):
    return values - jnp.sin(2.0 * math.pi * values) / (2.0 * math.pi)


def scale_table(channel_mean):
    ratios = jnp.arange(GRID, dtype=jnp.float32) / GRID
    raw = jnp.exp(ratios[:, None] * jnp.log(channel_mean)[None, :])
    top = jnp.max(raw, axis=1, keepdims=True)
    bottom = jnp.min(raw, axis=1, keepdims=True)
    return raw / jnp.sqrt(top * bottom)


def on_device(activations, weight):
    widened = gather_directly(activations, "tensor", 1)
    gathered = lax.all_gather(widened, DP, axis=0, tiled=True)
    columns = lax.all_to_all(weight, DP, split_axis=1, concat_axis=0, tiled=True)
    width = columns.shape[1]
    token_count = gathered.shape[0]
    channel_mean = jnp.sum(jnp.abs(gathered), axis=0, dtype=jnp.float32) / token_count + 1e-06
    scales = scale_table(channel_mean)
    base_out = jnp.dot(gathered, columns, preferred_element_type=jnp.float32)
    weight_float = columns.astype(jnp.float32)

    def local_error(factor):
        scaled = weight_float * factor[:, None]
        grouped = scaled.reshape(D // GROUP, GROUP, width)
        quant_step = (jnp.max(jnp.abs(grouped), axis=1, keepdims=True) + 1e-06) / 7.0
        levels = soft_round(grouped / quant_step)
        dequant = ((levels * quant_step).reshape(D, width) / factor[:, None]).astype(jnp.bfloat16)
        quant_out = jnp.dot(gathered, dequant, preferred_element_type=jnp.float32)
        residue = quant_out - base_out
        return jnp.sum(residue * residue, axis=0)

    column_sums = lax.map(local_error, scales)
    totals = by_axis(jnp.sum(column_sums, axis=1), DP_TENSOR)
    errors = totals / (token_count * F)
    column_errors = column_sums / token_count
    rows = D // lax.axis_size(DP)
    own_mean = lax.dynamic_slice_in_dim(channel_mean, lax.axis_index(DP) * rows, rows)
    return (own_mean, column_errors, errors)


def solution(mesh):
    torus = Mesh(
        mesh.devices.reshape(4, 8, 2, mesh.shape["tensor"]), ("dp_0", "dp_1", "dp_2", "tensor")
    )
    placed = (P(DP, "tensor"), P(DP, "tensor"))
    return jax.shard_map(
        on_device,
        mesh=torus,
        in_specs=placed,
        out_specs=(P(DP), P(None, TENSOR_DP), P()),
        check_vma=False,
    )
```

profile of v0, /device:TPU:2, one launch (start us, length us, event | category | flops | bytes accessed | tf_op | source)
XLA Modules:
  0.0 334.3 jit_solution(7435003003157472509)
XLA Ops:
  7.2 0.0 all-gather.3.cloned.1.call-start
  7.2 0.9 broadcast_in_dim.7
  8.1 10.9 %all_to_all.24 = bf16[4,12,2048]{2,1,0:T(8,128)(2,1)S(1)} all-to-all(bf16[4,12,2048]{2,1,0:T(8,128)(2,1)S(1)} %broadcast_in_dim.7), channel_id=1, replica_groups=mesh['dp_0'=4,'dp_1'=8,'dp_2'=2,'tensor'=4] {'tensor'}, dimensions={0} | all-to-all | bytes 393216 | tf_op jit(solution)/shard_map/all_to_all | solution.py:26
  19.0 0.2 copy.13
  19.2 0.8 reshape.54
  20.0 0.0 all-gather.3.cloned.1.call-update
  20.0 3.9 %copy.14 = bf16[128,7168]{0,1:T(8,128)(2,1)} copy(bf16[128,7168]{1,0:T(8,128)(2,1)} %param.5) | data formatting | bytes 3670016 | tf_op args[1]
  23.9 12.0 %all-to-all-start.1 = ((bf16[128,64,112]{0,2,1:T(8,128)(2,1)}), bf16[128,64,112]{0,2,1:T(8,128)(2,1)S(1)}, u32[]{:S(2)}, u32[]{:S(2)}) async-start(bf16[128,64,112]{0,2,1:T(8,128)(2,1)} %bitcast.7), calls=%async_computation.1 | async-start | bytes 3670016 | tf_op jit(solution)/shard_map/all_to_all | solution.py:54
  36.0 52.4 %all-to-all-done.1 = bf16[128,64,112]{0,2,1:T(8,128)(2,1)S(1)} async-done(((bf16[128,64,112]{0,2,1:T(8,128)(2,1)}), bf16[128,64,112]{0,2,1:T(8,128)(2,1)S(1)}, u32[]{:S(2)}, u32[]{:S(2)}) %all-to-all-start.1) | async-done | bytes 1835040 | tf_op jit(solution)/shard_map/all_to_all | solution.py:54
  88.4 2.1 bitcast_convert_fusion
  90.5 5.4 %copy.16 = f32[8192,112]{1,0:T(8,128)} copy(f32[8192,112]{0,1:T(8,128)} %bitcast_convert_fusion) | data formatting | bytes 7340032 | tf_op jit(solution)/shard_map/while | solution.py:72
  96.0 36.0 %all-gather.3.cloned.1.call-done = bf16[64,12,8192]{2,1,0:T(8,128)(2,1)} async-done(((bf16[1,12,8192]{2,1,0:T(8,128)(2,1)}), bf16[64,12,8192]{2,1,0:T(8,128)(2,1)}) %all-gather.3.cloned.1.call-update) | async-done | bytes 12582928 | tf_op jit(solution)/shard_map/all_gather | solution.py:53
  131.9 16.8 %reshape.55 = bf16[768,8192]{1,0:T(8,128)(2,1)} reshape(bf16[64,12,8192]{2,1,0:T(8,128)(2,1)} %all-gather.3.cloned.1.call-done) | data formatting | bytes 25165824
  148.8 7.6 %convert_reduce_fusion = f32[8192]{0:T(1024)S(1)} fusion(bf16[768,8192]{1,0:T(8,128)(2,1)} %reshape.55), kind=kLoop, calls=%fused_computation.11 | loop fusion | flops 18866176 | bytes 12615680 | tf_op jit(solution)/shard_map/reduce_sum | solution.py:57
  156.5 0.3 fusion.9
  156.7 0.1 fusion.8
  156.9 8.7 %fusion.5 = f32[768,112]{0,1:T(8,128)S(1)} fusion(bf16[768,8192]{1,0:T(8,128)(2,1)} %reshape.55, bf16[128,64,112]{0,2,1:T(8,128)(2,1)S(1)} %all-to-all-done.1), kind=kOutput, calls=%fused_computation.12 | convolution fusion | flops 1409286144 | bytes 14761984 | tf_op jit(solution)/shard_map/dot_general | solution.py:59
  165.6 122.5 %while.10 = (s32[]{:T(128)}, f32[4,112]{1,0:T(4,128)S(1)}, f32[4,8192]{1,0:T(4,128)S(1)}, f32[8192,112]{1,0:T(8,128)}, bf16[768,8192]{1,0:T(8,128)(2,1)}, /*index=5*/f32[768,112]{0,1:T(8,128)S(1)}, s32[]{:T(128)}, s32[]{:T(128)}) while((s32[]{:T(128)}, f32[4,112]{1,0:T(4,128)S(1)}, f32[4,8192]{1,0:T(4,128)S(1)}, f32[8192,112]{1,0:T(8,128)}, ...), condition=%wide.region_6.7_spmd, body=%wide.region_3.6_spmd.sunk | while | flops 1419643776 | bytes 38864320 | solution.py:72
  165.8 0.0 copy-start
  165.9 3.2 abs_reduce_fusion.2
  169.1 0.2 copy-done
  169.3 18.3 %fusion.24 = bf16[8192,112]{1,0:T(8,128)(2,1)S(1)} fusion(f32[8192,112]{1,0:T(8,128)S(1)} %copy-done, f32[64,112]{1,0:T(8,128)S(1)} %add_multiply_fusion.2, f32[8192]{0:T(1024)S(1)} %bitcast.55), kind=kLoop, calls=%fused_computation.3.clone.1 | loop fusion | flops 7340032 | bytes 5566464 | tf_op jit(solution)/shard_map/while/body/eval_jaxpr/convert_element_type | solution.py:67
  187.5 8.8 %fusion.25 = f32[112]{0:T(128)S(1)} fusion(f32[768,112]{0,1:T(8,128)S(1)} %get-tuple-element.130, bf16[8192,112]{1,0:T(8,128)(2,1)S(1)} %fusion.24, bf16[768,8192]{1,0:T(8,128)(2,1)} %get-tuple-element.129), kind=kOutput, calls=%fused_computation.8.clone.1 | convolution fusion | flops 1409544064 | bytes 14762432 | tf_op jit(solution)/shard_map/while/body/eval_jaxpr/dot_general | solution.py:68
  196.4 0.0 copy-start
  196.5 3.2 abs_reduce_fusion.2
  199.7 0.2 copy-done
  199.8 18.3 %fusion.24 = bf16[8192,112]{1,0:T(8,128)(2,1)S(1)} fusion(f32[8192,112]{1,0:T(8,128)S(1)} %copy-done, f32[64,112]{1,0:T(8,128)S(1)} %add_multiply_fusion.2, f32[8192]{0:T(1024)S(1)} %bitcast.55), kind=kLoop, calls=%fused_computation.3.clone.1 | loop fusion | flops 7340032 | bytes 5566464 | tf_op jit(solution)/shard_map/while/body/eval_jaxpr/convert_element_type | solution.py:67
  218.1 8.8 %fusion.25 = f32[112]{0:T(128)S(1)} fusion(f32[768,112]{0,1:T(8,128)S(1)} %get-tuple-element.130, bf16[8192,112]{1,0:T(8,128)(2,1)S(1)} %fusion.24, bf16[768,8192]{1,0:T(8,128)(2,1)} %get-tuple-element.129), kind=kOutput, calls=%fused_computation.8.clone.1 | convolution fusion | flops 1409544064 | bytes 14762432 | tf_op jit(solution)/shard_map/while/body/eval_jaxpr/dot_general | solution.py:68
  227.0 0.0 copy-start
  227.0 3.2 abs_reduce_fusion.2
  230.2 0.2 copy-done
  230.4 18.3 %fusion.24 = bf16[8192,112]{1,0:T(8,128)(2,1)S(1)} fusion(f32[8192,112]{1,0:T(8,128)S(1)} %copy-done, f32[64,112]{1,0:T(8,128)S(1)} %add_multiply_fusion.2, f32[8192]{0:T(1024)S(1)} %bitcast.55), kind=kLoop, calls=%fused_computation.3.clone.1 | loop fusion | flops 7340032 | bytes 5566464 | tf_op jit(solution)/shard_map/while/body/eval_jaxpr/convert_element_type | solution.py:67
  248.7 8.8 %fusion.25 = f32[112]{0:T(128)S(1)} fusion(f32[768,112]{0,1:T(8,128)S(1)} %get-tuple-element.130, bf16[8192,112]{1,0:T(8,128)(2,1)S(1)} %fusion.24, bf16[768,8192]{1,0:T(8,128)(2,1)} %get-tuple-element.129), kind=kOutput, calls=%fused_computation.8.clone.1 | convolution fusion | flops 1409544064 | bytes 14762432 | tf_op jit(solution)/shard_map/while/body/eval_jaxpr/dot_general | solution.py:68
  257.6 0.0 copy-start
  257.6 3.2 abs_reduce_fusion.2
  260.8 0.2 copy-done
  261.0 18.3 %fusion.24 = bf16[8192,112]{1,0:T(8,128)(2,1)S(1)} fusion(f32[8192,112]{1,0:T(8,128)S(1)} %copy-done, f32[64,112]{1,0:T(8,128)S(1)} %add_multiply_fusion.2, f32[8192]{0:T(1024)S(1)} %bitcast.55), kind=kLoop, calls=%fused_computation.3.clone.1 | loop fusion | flops 7340032 | bytes 5566464 | tf_op jit(solution)/shard_map/while/body/eval_jaxpr/convert_element_type | solution.py:67
  279.3 8.8 %fusion.25 = f32[112]{0:T(128)S(1)} fusion(f32[768,112]{0,1:T(8,128)S(1)} %get-tuple-element.130, bf16[8192,112]{1,0:T(8,128)(2,1)S(1)} %fusion.24, bf16[768,8192]{1,0:T(8,128)(2,1)} %get-tuple-element.129), kind=kOutput, calls=%fused_computation.8.clone.1 | convolution fusion | flops 1409544064 | bytes 14762432 | tf_op jit(solution)/shard_map/while/body/eval_jaxpr/dot_general | solution.py:68
  288.1 0.7 fusion.12
  288.8 9.1 %psum.28 = f32[4]{0:T(128)S(1)} all-reduce(f32[4]{0:T(128)S(1)} %get-tuple-element.70), channel_id=1, replica_groups=mesh['dp_0'=4,'dp_1'=8,'dp_2'=2,'tensor'=4] {'dp_0'}, use_global_device_ids=true, to_apply=%region_8.9 | all-reduce | flops 4 | bytes 32 | tf_op jit(solution)/shard_map/psum | solution.py:36
  298.0 15.8 %psum.29 = f32[4]{0:T(128)S(1)} all-reduce(f32[4]{0:T(128)S(1)} %psum.28), channel_id=1, replica_groups=mesh['dp_0'=4,'dp_1'=8,'dp_2'=2,'tensor'=4] {'dp_1'}, use_global_device_ids=true, to_apply=%region_9.10 | all-reduce | flops 4 | bytes 32 | tf_op jit(solution)/shard_map/psum | solution.py:36
  313.7 2.5 psum.30
  316.2 10.2 %psum.31 = f32[4]{0:T(128)S(1)} all-reduce(f32[4]{0:T(128)S(1)} %psum.30), channel_id=1, replica_groups=mesh['dp_0'=4,'dp_1'=8,'dp_2'=2,'tensor'=4] {'tensor'}, use_global_device_ids=true, to_apply=%region_11.12 | all-reduce | flops 4 | bytes 32 | tf_op jit(solution)/shard_map/psum | solution.py:36
  326.3 0.5 broadcast_multiply_fusion.1
  326.9 0.6 dynamic_slice.7
  (16 shorter events, 0.4 us)
Async XLA Ops:
  7.2 124.8 %all-gather.3.cloned.1.call-start = ((), (), s32[]{:S(2)}) async-start(), calls=%async_computation.2 | async-start | bytes 17039360 | tf_op jit(solution)/shard_map/all_gather | solution.py:53
  23.9 64.5 %all-to-all-start.1 = ((bf16[128,64,112]{0,2,1:T(8,128)(2,1)}), bf16[128,64,112]{0,2,1:T(8,128)(2,1)S(1)}, u32[]{:S(2)}, u32[]{:S(2)}) async-start(bf16[128,64,112]{0,2,1:T(8,128)(2,1)} %bitcast.7), calls=%async_computation.1 | async-start | bytes 3670016 | tf_op jit(solution)/shard_map/all_to_all | solution.py:54
  165.8 3.5 %copy-start = (f32[8192,112]{1,0:T(8,128)S(1)}, f32[8192,112]{1,0:T(8,128)}, u32[]{:S(2)}) copy-start(f32[8192,112]{1,0:T(8,128)} %get-tuple-element.128) | copy-start | bytes 11010052 | tf_op jit(solution)/shard_map/while
  196.4 3.5 %copy-start = (f32[8192,112]{1,0:T(8,128)S(1)}, f32[8192,112]{1,0:T(8,128)}, u32[]{:S(2)}) copy-start(f32[8192,112]{1,0:T(8,128)} %get-tuple-element.128) | copy-start | bytes 11010052 | tf_op jit(solution)/shard_map/while
  227.0 3.5 %copy-start = (f32[8192,112]{1,0:T(8,128)S(1)}, f32[8192,112]{1,0:T(8,128)}, u32[]{:S(2)}) copy-start(f32[8192,112]{1,0:T(8,128)} %get-tuple-element.128) | copy-start | bytes 11010052 | tf_op jit(solution)/shard_map/while
  257.6 3.5 %copy-start = (f32[8192,112]{1,0:T(8,128)S(1)}, f32[8192,112]{1,0:T(8,128)}, u32[]{:S(2)}) copy-start(f32[8192,112]{1,0:T(8,128)} %get-tuple-element.128) | copy-start | bytes 11010052 | tf_op jit(solution)/shard_map/while
Sparse Core Ops, SparseCore 0:
  20.1 111.7 all-gather.2
where the time goes:
time: 335 us; the launch traced here: 334 us
  other arithmetic  97.2 us (29%)
  waiting for transfers between devices  88.4 us (26%)
  blocking collectives  48.5 us (14%)
  matrix products  44 us (13%)
  local copies, waits for them, and re-layouts  29.7 us (9%)
  between operations  14.1 us (4%)
  starting transfers between devices  12.1 us (4%)
    convert_element_type x4, other arithmetic, local_error(): ((levels * quant_step).reshape(D, width) / factor[:, None]).astype(jnp.bf...  73 us
    all_to_all x1, waiting for transfers between devices, on_device(): lax.all_to_all(weight, DP, split_axis=1, concat_axis=0, tiled=True)  52.4 us
    psum x4, blocking collectives, by_axis(): return functools.reduce(lax.psum, axes, shard)  37.5 us
    all_gather x1, waiting for transfers between devices, on_device(): gathered = lax.all_gather(widened, DP, axis=0, tiled=True)  36 us
    dot_general x4, matrix products, local_error(): quant_out = jnp.dot(gathered, dequant, preferred_element_type=jnp.float32)  35.2 us
    unnamed x3, local copies, waits for them, and re-layouts  21.6 us
    reduce_max x4, other arithmetic, local_error(): jnp.max(jnp.abs(grouped), axis=1, keepdims=True) + 1e-06  12.7 us
    all_to_all x1, starting transfers between devices, on_device(): lax.all_to_all(weight, DP, split_axis=1, concat_axis=0, tiled=True)  12 us
  transfers between devices with their start and end apart: 2, of which 2 were waited for; matrix products, arithmetic and copies ran while one was open for 3% of the time, Pallas kernels for 0%

commit v1 on v0

--- a/solution.py
+++ b/solution.py
@@ -50,7 +50,9 @@
 
 def on_device(activations, weight):
     widened = gather_directly(activations, "tensor", 1)
-    gathered = lax.all_gather(widened, DP, axis=0, tiled=True)
+    gathered = jnp.concatenate(
+        lax.all_to_all(jnp.stack([widened] * lax.axis_size(DP)), DP, 0, 0), axis=0
+    )
     columns = lax.all_to_all(weight, DP, split_axis=1, concat_axis=0, tiled=True)
     width = columns.shape[1]
     token_count = gathered.shape[0]

time: 335 us -> 642 us (1.92)
  waiting for transfers between devices: 88.4 us -> 404 us
  blocking collectives: 48.5 us -> 33.9 us
  between operations: 14.1 us -> 0.73 us
  starting transfers between devices: 12.1 us -> 24.1 us
  local copies, waits for them, and re-layouts: 29.7 us -> 36.3 us
    all_to_all x0 -> x2, waiting for transfers between devices: none -> 360 us  [the longest x1 358 us: on_device(): lax.all_to_all(jnp.stack([widened] * lax.axis_size(DP)), DP, 0, 0)]
    all_gather x1 -> x0, waiting for transfers between devices: 36 us -> none  [on_device(): gathered = lax.all_gather(widened, DP, axis=0, tiled=True)]
    unnamed x3, local copies, waits for them, and re-layouts: 21.6 us -> 4.16 us
    reshape x0 -> x1, local copies, waits for them, and re-layouts: none -> 16.9 us  [on_device(): jnp.concatenate(lax.all_to_all(jnp.stack([widened] * lax.axis_size(DP)),...]
    all_to_all x0 -> x2, starting transfers between devices: none -> 12.1 us  [the longest x1 7.64 us: on_device(): lax.all_to_all(jnp.stack([widened] * lax.axis_size(DP)), DP, 0, 0)]
    all_to_all x1 -> x0, blocking collectives: 10.9 us -> none  [from_everyone(): lax.all_to_all(jnp.broadcast_to(shard[None], (devices, *shard.shape)), ax...]
    all_to_all x1, waiting for transfers between devices: 52.4 us -> 43.5 us  [on_device(): lax.all_to_all(weight, DP, split_axis=1, concat_axis=0, tiled=True)]
  transfers between devices with their start and end apart: 2 -> 3, of which waited for: 2 -> 3; matrix products, arithmetic and copies ran while one was open for 3% -> 2% of each run, Pallas kernels for 0% -> 0%
where the time goes in v1:
time: 642 us; the launch traced here: 639 us
  waiting for transfers between devices  404 us (63%)
  other arithmetic  96.3 us (15%)
  matrix products  44 us (7%)
  local copies, waits for them, and re-layouts  36.3 us (6%)
  blocking collectives  33.9 us (5%)
  starting transfers between devices  24.1 us (4%)
    all_to_all x1, waiting for transfers between devices, on_device(): lax.all_to_all(jnp.stack([widened] * lax.axis_size(DP)), DP, 0, 0)  358 us
    convert_element_type x4, other arithmetic, local_error(): ((levels * quant_step).reshape(D, width) / factor[:, None]).astype(jnp.bf...  73 us
    all_to_all x1, waiting for transfers between devices, on_device(): lax.all_to_all(weight, DP, split_axis=1, concat_axis=0, tiled=True)  43.5 us
    dot_general x4, matrix products, local_error(): quant_out = jnp.dot(gathered, dequant, preferred_element_type=jnp.float32)  35.2 us
    psum x4, blocking collectives, by_axis(): return functools.reduce(lax.psum, axes, shard)  33.9 us
    reshape x1, local copies, waits for them, and re-layouts, on_device(): jnp.concatenate(lax.all_to_all(jnp.stack([widened] * lax.axis_size(DP)),...  16.9 us
  transfers between devices with their start and end apart: 3, of which 3 were waited for; matrix products, arithmetic and copies ran while one was open for 2% of the time, Pallas kernels for 0%

profile of v1, /device:TPU:2, one launch (start us, length us, event | category | flops | bytes accessed | tf_op | source)
XLA Modules:
  0.0 639.5 jit_solution(4678732688074810310)
XLA Ops:
  0.6 1.6 broadcast_in_dim.7
  2.2 4.5 all-to-all-start
  6.7 3.9 copy.14
  10.6 2.8 all-to-all-done
  13.3 12.0 %all-to-all-start.2 = ((bf16[128,64,112]{0,2,1:T(8,128)(2,1)}), bf16[128,64,112]{0,2,1:T(8,128)(2,1)S(1)}, u32[]{:S(2)}, u32[]{:S(2)}) async-start(bf16[128,64,112]{0,2,1:T(8,128)(2,1)} %bitcast.7), calls=%async_computation.2 | async-start | bytes 3670016 | tf_op jit(solution)/shard_map/all_to_all | solution.py:56
  25.4 0.2 copy.13
  25.5 0.1 pad
  25.6 0.2 copy.18
  25.8 43.5 %all-to-all-done.2 = bf16[128,64,112]{0,2,1:T(8,128)(2,1)S(1)} async-done(((bf16[128,64,112]{0,2,1:T(8,128)(2,1)}), bf16[128,64,112]{0,2,1:T(8,128)(2,1)S(1)}, u32[]{:S(2)}, u32[]{:S(2)}) %all-to-all-start.2) | async-done | bytes 1835040 | tf_op jit(solution)/shard_map/all_to_all | solution.py:56
  69.3 5.9 stack.3
  75.2 7.6 %all-to-all-start.1 = ((bf16[64,12,8192]{2,1,0:T(8,128)(2,1)}), bf16[64,12,8192]{2,1,0:T(8,128)(2,1)}, u32[]{:S(2)}, u32[]{:S(2)}) async-start(bf16[64,12,8192]{2,1,0:T(8,128)(2,1)} %stack.3), calls=%async_computation.1 | async-start | bytes 33554432 | tf_op jit(solution)/shard_map/all_to_all | solution.py:54
  82.9 2.1 bitcast_convert_fusion
  85.0 5.4 copy.16
  90.4 357.6 %all-to-all-done.1 = bf16[64,12,8192]{2,1,0:T(8,128)(2,1)} async-done(((bf16[64,12,8192]{2,1,0:T(8,128)(2,1)}), bf16[64,12,8192]{2,1,0:T(8,128)(2,1)}, u32[]{:S(2)}, u32[]{:S(2)}) %all-to-all-start.1) | async-done | bytes 12582944 | tf_op jit(solution)/shard_map/all_to_all | solution.py:54
  448.0 7.4 %convert_reduce_fusion = f32[8192]{0:T(1024)S(1)} fusion(bf16[64,12,8192]{2,1,0:T(8,128)(2,1)} %all-to-all-done.1), kind=kLoop, calls=%fused_computation.11 | loop fusion | flops 18866176 | bytes 12615680 | tf_op jit(solution)/shard_map/reduce_sum | solution.py:59
  455.4 0.3 fusion.9
  455.7 0.1 fusion.8
  455.8 16.9 %reshape.55 = bf16[768,8192]{1,0:T(8,128)(2,1)} reshape(bf16[64,12,8192]{2,1,0:T(8,128)(2,1)} %all-to-all-done.1) | data formatting | bytes 25165824 | tf_op jit(solution)/shard_map/reshape | solution.py:53
  472.7 8.7 %fusion.5 = f32[768,112]{0,1:T(8,128)S(1)} fusion(bf16[768,8192]{1,0:T(8,128)(2,1)} %reshape.55, bf16[128,64,112]{0,2,1:T(8,128)(2,1)S(1)} %all-to-all-done.2), kind=kOutput, calls=%fused_computation.12 | convolution fusion | flops 1409286144 | bytes 14761984 | tf_op jit(solution)/shard_map/dot_general | solution.py:61
  481.4 122.3 %while.10 = (s32[]{:T(128)}, f32[4,112]{1,0:T(4,128)S(1)}, f32[4,8192]{1,0:T(4,128)S(1)}, f32[8192,112]{1,0:T(8,128)}, bf16[768,8192]{1,0:T(8,128)(2,1)}, /*index=5*/f32[768,112]{0,1:T(8,128)S(1)}, s32[]{:T(128)}, s32[]{:T(128)}) while((s32[]{:T(128)}, f32[4,112]{1,0:T(4,128)S(1)}, f32[4,8192]{1,0:T(4,128)S(1)}, f32[8192,112]{1,0:T(8,128)}, ...), condition=%wide.region_6.7_spmd, body=%wide.region_3.6_spmd.sunk | while | flops 1419643776 | bytes 38864312 | solution.py:74
  481.4 0.0 copy-start
  481.5 3.0 abs_reduce_fusion.2
  484.5 0.3 copy-done
  484.9 18.3 %fusion.24 = bf16[8192,112]{1,0:T(8,128)(2,1)S(1)} fusion(f32[8192,112]{1,0:T(8,128)S(1)} %copy-done, f32[64,112]{1,0:T(8,128)S(1)} %add_multiply_fusion.2, f32[8192]{0:T(1024)S(1)} %bitcast.58), kind=kLoop, calls=%fused_computation.3.clone.1 | loop fusion | flops 7340032 | bytes 5566464 | tf_op jit(solution)/shard_map/while/body/eval_jaxpr/convert_element_type | solution.py:69
  503.1 8.8 %fusion.25 = f32[112]{0:T(128)S(1)} fusion(f32[768,112]{0,1:T(8,128)S(1)} %get-tuple-element.130, bf16[8192,112]{1,0:T(8,128)(2,1)S(1)} %fusion.24, bf16[768,8192]{1,0:T(8,128)(2,1)} %get-tuple-element.129), kind=kOutput, calls=%fused_computation.8.clone.1 | convolution fusion | flops 1409544064 | bytes 14762432 | tf_op jit(solution)/shard_map/while/body/eval_jaxpr/dot_general | solution.py:70
  512.0 0.0 copy-start
  512.0 3.0 abs_reduce_fusion.2
  515.1 0.3 copy-done
  515.4 18.3 %fusion.24 = bf16[8192,112]{1,0:T(8,128)(2,1)S(1)} fusion(f32[8192,112]{1,0:T(8,128)S(1)} %copy-done, f32[64,112]{1,0:T(8,128)S(1)} %add_multiply_fusion.2, f32[8192]{0:T(1024)S(1)} %bitcast.58), kind=kLoop, calls=%fused_computation.3.clone.1 | loop fusion | flops 7340032 | bytes 5566464 | tf_op jit(solution)/shard_map/while/body/eval_jaxpr/convert_element_type | solution.py:69
  533.7 8.8 %fusion.25 = f32[112]{0:T(128)S(1)} fusion(f32[768,112]{0,1:T(8,128)S(1)} %get-tuple-element.130, bf16[8192,112]{1,0:T(8,128)(2,1)S(1)} %fusion.24, bf16[768,8192]{1,0:T(8,128)(2,1)} %get-tuple-element.129), kind=kOutput, calls=%fused_computation.8.clone.1 | convolution fusion | flops 1409544064 | bytes 14762432 | tf_op jit(solution)/shard_map/while/body/eval_jaxpr/dot_general | solution.py:70
  542.6 0.0 copy-start
  542.6 3.0 abs_reduce_fusion.2
  545.7 0.3 copy-done
  546.0 18.3 %fusion.24 = bf16[8192,112]{1,0:T(8,128)(2,1)S(1)} fusion(f32[8192,112]{1,0:T(8,128)S(1)} %copy-done, f32[64,112]{1,0:T(8,128)S(1)} %add_multiply_fusion.2, f32[8192]{0:T(1024)S(1)} %bitcast.58), kind=kLoop, calls=%fused_computation.3.clone.1 | loop fusion | flops 7340032 | bytes 5566464 | tf_op jit(solution)/shard_map/while/body/eval_jaxpr/convert_element_type | solution.py:69
  564.3 8.8 %fusion.25 = f32[112]{0:T(128)S(1)} fusion(f32[768,112]{0,1:T(8,128)S(1)} %get-tuple-element.130, bf16[8192,112]{1,0:T(8,128)(2,1)S(1)} %fusion.24, bf16[768,8192]{1,0:T(8,128)(2,1)} %get-tuple-element.129), kind=kOutput, calls=%fused_computation.8.clone.1 | convolution fusion | flops 1409544064 | bytes 14762432 | tf_op jit(solution)/shard_map/while/body/eval_jaxpr/dot_general | solution.py:70
  573.1 0.0 copy-start
  573.2 3.0 abs_reduce_fusion.2
  576.3 0.3 copy-done
  576.6 18.3 %fusion.24 = bf16[8192,112]{1,0:T(8,128)(2,1)S(1)} fusion(f32[8192,112]{1,0:T(8,128)S(1)} %copy-done, f32[64,112]{1,0:T(8,128)S(1)} %add_multiply_fusion.2, f32[8192]{0:T(1024)S(1)} %bitcast.58), kind=kLoop, calls=%fused_computation.3.clone.1 | loop fusion | flops 7340032 | bytes 5566464 | tf_op jit(solution)/shard_map/while/body/eval_jaxpr/convert_element_type | solution.py:69
  594.9 8.8 %fusion.25 = f32[112]{0:T(128)S(1)} fusion(f32[768,112]{0,1:T(8,128)S(1)} %get-tuple-element.130, bf16[8192,112]{1,0:T(8,128)(2,1)S(1)} %fusion.24, bf16[768,8192]{1,0:T(8,128)(2,1)} %get-tuple-element.129), kind=kOutput, calls=%fused_computation.8.clone.1 | convolution fusion | flops 1409544064 | bytes 14762432 | tf_op jit(solution)/shard_map/while/body/eval_jaxpr/dot_general | solution.py:70
  603.7 0.7 fusion.12
  604.4 7.8 %psum.28 = f32[4]{0:T(128)S(1)} all-reduce(f32[4]{0:T(128)S(1)} %get-tuple-element.70), channel_id=1, replica_groups=mesh['dp_0'=4,'dp_1'=8,'dp_2'=2,'tensor'=4] {'dp_0'}, use_global_device_ids=true, to_apply=%region_8.9 | all-reduce | flops 4 | bytes 32 | tf_op jit(solution)/shard_map/psum | solution.py:36
  612.2 14.8 %psum.29 = f32[4]{0:T(128)S(1)} all-reduce(f32[4]{0:T(128)S(1)} %psum.28), channel_id=1, replica_groups=mesh['dp_0'=4,'dp_1'=8,'dp_2'=2,'tensor'=4] {'dp_1'}, use_global_device_ids=true, to_apply=%region_9.10 | all-reduce | flops 4 | bytes 32 | tf_op jit(solution)/shard_map/psum | solution.py:36
  627.0 2.5 psum.30
  629.5 8.9 %psum.31 = f32[4]{0:T(128)S(1)} all-reduce(f32[4]{0:T(128)S(1)} %psum.30), channel_id=1, replica_groups=mesh['dp_0'=4,'dp_1'=8,'dp_2'=2,'tensor'=4] {'tensor'}, use_global_device_ids=true, to_apply=%region_11.12 | all-reduce | flops 4 | bytes 32 | tf_op jit(solution)/shard_map/psum | solution.py:36
  638.4 0.5 broadcast_multiply_fusion.1
  638.9 0.6 dynamic_slice.7
  (16 shorter events, 0.4 us)
Async XLA Ops:
  2.2 11.1 %all-to-all-start = ((bf16[4,12,2048]{2,1,0:T(8,128)(2,1)}), bf16[4,12,2048]{2,1,0:T(8,128)(2,1)S(1)}, u32[]{:S(2)}, u32[]{:S(2)}) async-start(bf16[4,12,2048]{2,1,0:T(8,128)(2,1)} %broadcast_in_dim.7), calls=%async_computation | async-start | bytes 524288 | tf_op jit(solution)/shard_map/all_to_all | solution.py:26
  13.3 56.0 %all-to-all-start.2 = ((bf16[128,64,112]{0,2,1:T(8,128)(2,1)}), bf16[128,64,112]{0,2,1:T(8,128)(2,1)S(1)}, u32[]{:S(2)}, u32[]{:S(2)}) async-start(bf16[128,64,112]{0,2,1:T(8,128)(2,1)} %bitcast.7), calls=%async_computation.2 | async-start | bytes 3670016 | tf_op jit(solution)/shard_map/all_to_all | solution.py:56
  75.2 372.8 %all-to-all-start.1 = ((bf16[64,12,8192]{2,1,0:T(8,128)(2,1)}), bf16[64,12,8192]{2,1,0:T(8,128)(2,1)}, u32[]{:S(2)}, u32[]{:S(2)}) async-start(bf16[64,12,8192]{2,1,0:T(8,128)(2,1)} %stack.3), calls=%async_computation.1 | async-start | bytes 33554432 | tf_op jit(solution)/shard_map/all_to_all | solution.py:54
  481.4 3.5 copy-start
  512.0 3.5 copy-start
  542.6 3.5 copy-start
  573.1 3.5 copy-start
